TPU v7x, 256 devices: a 4x2x16 block of a 4x16x16 slice. The times are simulated.
256 devices in a mesh: groups: 2 (over y), tp: 16 (over z), tq: 4 (over x), tr: 2 (over core).
Axes of the slice: x: 4, y: 2, z: 16, core: 2. Of those that a mesh axis runs over, the one named last changes fastest.
The devices are a block of a 4x16x16 slice.
Arguments:
- attn_heads: bfloat16 [128, 16384], P('groups', ('tp', 'tq', 'tr')), parts along dimension 0, may hold values from -6 to 6
- residual: bfloat16 [128, 16384], P('groups', ('tp', 'tq', 'tr')), parts along dimension 0, may hold values from -120 to 120
- o_weight: bfloat16 [16384, 16384], P(('tp', 'tq', 'tr')), may hold values from -0.1875 to 0.1875
- norm_gain: bfloat16 [16384], P(('tp', 'tq', 'tr')), may hold values from 0.099609375 to 1.8984375
- q_weight: bfloat16 [16384, 16384], P(None, ('tp', 'tq', 'tr')), may hold values from -0.046875 to 0.046875
Outputs:
- hidden: bfloat16 [128, 16384], P('groups', ('tp', 'tq', 'tr')), parts along dimension 0
- peak_value: float32 [128], P('groups'), parts along dimension 0
- query: bfloat16 [128, 16384], P('groups', ('tp', 'tq', 'tr')), parts along dimension 0
There are 2 independent parts, one for each index of `groups`. A program takes and returns all parts, laid end to end along the dimension named above; an argument that names none is the same for every part. Nothing has to cross between parts.
All inputs are finite; a program needn't handle non-finite values. Where the computation divides by a largest or mean magnitude, that divisor is 1e-20 or more.
Results may differ from a plain program's by a relative error of at most 0.0095.
Values may be sent and summed in bfloat16 or wider, within the bound.
No kernel may reach another device: no remote copies, remote signals or barrier semaphores. Data moves between devices by JAX's collectives and lax.ppermute only.
A program may use at most 64 MiB of HBM per device.

v0:
```python
import jax
import jax.numpy as jnp
from jax import lax
from jax.sharding import PartitionSpec as P

D = 16384


def in_blocks(array, dim, devices):
    dims = array.shape
    tiles = array.reshape(*dims[:dim], devices, dims[dim] // devices, *dims[dim + 1 :])
    return jnp.moveaxis(tiles, dim, 0)


def summed_on_arrival(array, axis, dim):
    tiles = in_blocks(array, dim, lax.axis_size(axis))
    arrived = lax.all_to_all(tiles, axis, split_axis=0, concat_axis=0, tiled=True)
    return arrived.sum(axis=0)


def collected_together(array, axis):
    leaves = jax.tree.leaves(array)
    turns = sorted(range(len(leaves)), key=lambda k: -leaves[k].size)
    width = (1, *leaves[turns[0]].shape)[-1]
    lines = [
        jnp.pad(leaves[k].reshape(-1), (0, -leaves[k].size % width)).reshape(-1, width)
        for k in turns
    ]
    both, at, found = (lax.all_gather(jnp.concatenate(lines), axis), 0, {})
    for k, line in zip(turns, lines):
        share = both[:, at : at + len(line)].reshape(len(both), -1)
        found[k] = share[:, : leaves[k].size].reshape(-1, *leaves[k].shape)
        at += len(line)
    numbers = iter(range(len(leaves)))
    return jax.tree.map(lambda _: found[next(numbers)], array)


def joined_all(array, axes, combine):
    for axis in axes:
        pieces = collected_together(array, axis)
        array = jax.tree.map(lambda part: part[0], pieces)
        for k in range(1, lax.axis_size(axis)):
            array = combine(array, jax.tree.map(lambda part: part[k], pieces))
    return array


def laid_out(tiles, dim):
    tiles = jnp.moveaxis(tiles, 0, dim)
    dims = tiles.shape
    return tiles.reshape(*dims[:dim], dims[dim] * dims[dim + 1], *dims[dim + 2 :])


def from_everyone(array, axis):
    copies = jnp.broadcast_to(array, (lax.axis_size(axis), *array.shape))
    return lax.all_to_all(copies, axis, split_axis=0, concat_axis=0, tiled=True)


def collect(array, axis, dim):
    return laid_out(from_everyone(array, axis), dim)


def combine_stats(lhs_stats, rhs_stats):
    return (lhs_stats[0] + rhs_stats[0], jnp.maximum(lhs_stats[1], rhs_stats[1]))


def body(attn_heads, residual, o_weight, norm_gain, q_weight):
    terms = jnp.dot(attn_heads, o_weight, preferred_element_type=jnp.float32)
    section_one = lax.psum_scatter(terms, "tp", scatter_dimension=1, tiled=True)
    section_two = summed_on_arrival(section_one, "tq", 1)
    attn_total = summed_on_arrival(section_two, "tr", 1)
    hidden = (residual.astype(jnp.float32) + attn_total).astype(jnp.bfloat16)
    widened = hidden.astype(jnp.float32)
    gained = widened * norm_gain.astype(jnp.float32)
    squares = jnp.sum(widened * widened, axis=1)
    local_top = jnp.max(jnp.abs(gained), axis=1)
    row_total, global_top = joined_all((squares, local_top), ("tp", "tq", "tr"), combine_stats)
    inv_rms = lax.rsqrt(row_total / D + 1e-05)
    normed = gained * inv_rms[:, None]
    peak_value = global_top * inv_rms
    quantized = (normed * (448.0 / (peak_value + 1e-06))[:, None]).astype(jnp.bfloat16)
    gathered_two = collect(quantized, "tr", 1)
    gathered_four = collect(gathered_two, "tq", 1)
    projected = jnp.dot(
        lax.all_gather(gathered_four, "tp", axis=1, tiled=True),
        q_weight,
        preferred_element_type=jnp.float32,
    )
    query = (projected * ((peak_value + 1e-06) / 448.0)[:, None]).astype(jnp.bfloat16)
    return (hidden, peak_value, query)


def solution(mesh):
    placed = (
        P("groups", ("tp", "tq", "tr")),
        P("groups", ("tp", "tq", "tr")),
        P(("tp", "tq", "tr"), None),
        P(("tp", "tq", "tr")),
        P(None, ("tp", "tq", "tr")),
    )
    return jax.shard_map(
        body,
        mesh=mesh,
        in_specs=placed,
        out_specs=(P("groups", ("tp", "tq", "tr")), P("groups"), P("groups", ("tp", "tq", "tr"))),
        check_vma=False,
    )
```

profile of v0, /device:TPU:34, one launch (start us, length us, event | category | flops | bytes accessed | tf_op | source)
XLA Modules:
  0.0 252.2 jit_solution(817903353825983854)
XLA Ops:
  7.2 0.0 copy-start
  7.2 0.1 reduce-scatter.2.cloned.1.call-start
  7.3 0.6 copy-done
  7.9 4.8 %fusion.15 = f32[64,16384]{1,0:T(8,128)} fusion(bf16[64,128]{1,0:T(8,128)(2,1)S(1)} %copy-done, bf16[128,16384]{1,0:T(8,128)(2,1)} %param.7), kind=kOutput, calls=%fused_computation.64 | convolution fusion | flops 268435456 | bytes 8404992 | tf_op jit(solution)/shard_map/dot_general | solution.py:67
  12.7 0.1 reduce-scatter.2.cloned.1.call-update
  12.8 92.7 %reduce-scatter.2.cloned.1.call-done = f32[64,1024]{1,0:T(8,128)} async-done(((f32[64,16384]{1,0:T(8,128)}), f32[64,1024]{1,0:T(8,128)}) %reduce-scatter.2.cloned.1.call-update) | async-done | bytes 262160 | tf_op jit(solution)/shard_map/reduce_scatter | solution.py:68
  105.5 1.7 copy.20
  107.1 5.0 %all-to-all-start = ((f32[4,64,256]{2,1,0:T(8,128)}), f32[4,64,256]{2,1,0:T(8,128)S(1)}, u32[]{:S(2)}, u32[]{:S(2)}) async-start(f32[4,64,256]{2,1,0:T(8,128)} %bitcast.44), calls=%async_computation.1 | async-start | bytes 524288 | tf_op jit(solution)/shard_map/all_to_all | solution.py:17
  112.2 5.2 %all-to-all-done = f32[4,64,256]{2,1,0:T(8,128)S(1)} async-done(((f32[4,64,256]{2,1,0:T(8,128)}), f32[4,64,256]{2,1,0:T(8,128)S(1)}, u32[]{:S(2)}, u32[]{:S(2)}) %all-to-all-start) | async-done | bytes 262176 | tf_op jit(solution)/shard_map/all_to_all | solution.py:17
  117.5 3.8 %all_to_all.20 = f32[2,64,128]{2,1,0:T(8,128)S(1)} all-to-all(f32[2,64,128]{2,1,0:T(8,128)S(1)} %copy.12), channel_id=1, replica_groups=mesh['groups'=2,'tp'=16,'tq'=4,'tr'=2] {'tr'}, dimensions={0} | all-to-all | bytes 131072 | tf_op jit(solution)/shard_map/all_to_all | solution.py:17
  121.3 0.0 copy-done.2
  121.3 0.1 fusion.6
  121.4 0.0 copy-start.1
  121.4 27.3 %all-gather.3 = f32[16,2,64]{2,1,0:T(2,128)S(1)} all-gather(f32[1,2,64]{2,1,0:T(2,128)S(1)} %maximum_bitcast_fusion), channel_id=2, replica_groups=mesh['groups'=2,'tp'=16,'tq'=4,'tr'=2] {'tp'}, dimensions={0}, use_global_device_ids=true | all-gather | bytes 8704 | tf_op jit(solution)/shard_map/all_gather | solution.py:29
  148.7 8.5 %all-gather.4 = f32[4,2,64]{2,1,0:T(2,128)S(1)} all-gather(f32[1,2,64]{2,1,0:T(2,128)S(1)} %maximum_bitcast_fusion.1), channel_id=3, replica_groups=mesh['groups'=2,'tp'=16,'tq'=4,'tr'=2] {'tq'}, dimensions={0}, use_global_device_ids=true | all-gather | bytes 2560 | tf_op jit(solution)/shard_map/all_gather | solution.py:29
  157.3 1.9 all-gather.5
  159.1 0.0 copy-start.3
  159.2 0.1 fusion.5
  159.3 3.8 %all_to_all.21 = bf16[2,64,128]{2,1,0:T(8,128)(2,1)S(1)} all-to-all(bf16[2,64,128]{2,1,0:T(8,128)(2,1)S(1)} %broadcast_in_dim.4), channel_id=1, replica_groups=mesh['groups'=2,'tp'=16,'tq'=4,'tr'=2] {'tr'}, dimensions={0} | all-to-all | bytes 65536 | tf_op jit(solution)/shard_map/all_to_all | solution.py:55
  163.0 8.1 %all_to_all.22 = bf16[4,64,256]{2,1,0:T(8,128)(2,1)S(1)} all-to-all(bf16[4,64,256]{2,1,0:T(8,128)(2,1)S(1)} %broadcast_in_dim.5), channel_id=1, replica_groups=mesh['groups'=2,'tp'=16,'tq'=4,'tr'=2] {'tq'}, dimensions={0} | all-to-all | bytes 262144 | tf_op jit(solution)/shard_map/all_to_all | solution.py:55
  171.1 0.7 copy.17
  171.8 0.1 all-gather.8.cloned.1.call-update
  171.9 69.2 %all-gather.8.cloned.1.call-done = bf16[64,16384]{1,0:T(8,128)(2,1)} async-done(((bf16[64,1024]{1,0:T(8,128)(2,1)}), bf16[64,16384]{1,0:T(8,128)(2,1)}) %all-gather.8.cloned.1.call-update) | async-done | bytes 2097168 | tf_op jit(solution)/shard_map/all_gather | solution.py:84
  241.1 4.3 %fusion = bf16[64,128]{1,0:T(8,128)(2,1)} fusion(bf16[64,16384]{1,0:T(8,128)(2,1)} %all-gather.8.cloned.1.call-done, bf16[16384,128]{1,0:T(8,128)(2,1)} %param.9, f32[64]{0:T(128)S(1)} %get-tuple-element.5), kind=kOutput, calls=%fused_computation.1 | convolution fusion | flops 268451840 | bytes 6308096 | tf_op jit(solution)/shard_map/dot_general | solution.py:83
  (22 shorter events, 0.2 us)
Async XLA Ops:
  7.2 0.7 copy-start
  7.2 98.3 %reduce-scatter.2.cloned.1.call-start = ((), (), s32[]{:S(2)}) async-start(), calls=%async_computation.5 | async-start | bytes 4456448 | tf_op jit(solution)/shard_map/reduce_scatter | solution.py:68
  12.7 99.4 %copy-start.4 = (bf16[128]{0:T(256)(128)(2,1)S(1)}, bf16[128]{0:T(256)(128)(2,1)}, u32[]{:S(2)}) copy-start(bf16[128]{0:T(256)(128)(2,1)} %param.8) | copy-start | bytes 772
  12.7 108.5 %copy-start.2 = (bf16[64,128]{1,0:T(8,128)(2,1)S(1)}, bf16[64,128]{1,0:T(8,128)(2,1)}, u32[]{:S(2)}) copy-start(bf16[64,128]{1,0:T(8,128)(2,1)} %param.6) | copy-start | bytes 49156
  107.1 10.3 %all-to-all-start = ((f32[4,64,256]{2,1,0:T(8,128)}), f32[4,64,256]{2,1,0:T(8,128)S(1)}, u32[]{:S(2)}, u32[]{:S(2)}) async-start(f32[4,64,256]{2,1,0:T(8,128)} %bitcast.44), calls=%async_computation.1 | async-start | bytes 524288 | tf_op jit(solution)/shard_map/all_to_all | solution.py:17
  112.2 128.9 %all-gather.8.cloned.1.call-start = ((), (), s32[]{:S(2)}) async-start(), calls=%async_computation.6 | async-start | bytes 2228224 | tf_op jit(solution)/shard_map/all_gather | solution.py:84
  121.4 124.0 %copy-start.1 = (bf16[64,128]{1,0:T(8,128)(2,1)}, bf16[64,128]{1,0:T(8,128)(2,1)S(1)}, u32[]{:S(2)}) copy-start(bf16[64,128]{1,0:T(8,128)(2,1)S(1)} %get-tuple-element.8) | copy-start | bytes 49156
  159.1 86.2 %copy-start.3 = (f32[64]{0:T(128)}, f32[64]{0:T(128)S(1)}, u32[]{:S(2)}) copy-start(f32[64]{0:T(128)S(1)} %get-tuple-element.6) | copy-start | bytes 772
Sparse Core Ops, SparseCore 0:
  12.9 92.5 reduce-scatter.1
  172.0 69.0 all-gather.7
where the time goes:
time: 253 us; the launch traced here: 252 us
  waiting for transfers between devices  167 us (66%)
  blocking collectives  53.3 us (21%)
  between operations  14.2 us (6%)
  matrix products  9.1 us (4%)
  starting transfers between devices  5.09 us (2%)
  local copies, waits for them, and re-layouts  3.06 us (1%)
    reduce_scatter x1, waiting for transfers between devices, body(): section_one = lax.psum_scatter(terms, 'tp', scatter_dimension=1, tiled=True)  92.7 us
    all_gather x1, waiting for transfers between devices, body(): lax.all_gather(gathered_four, 'tp', axis=1, tiled=True)  69.2 us
    all_gather x3, blocking collectives, collected_together(): both, at, found = (lax.all_gather(jnp.concatenate(lines), axis), 0, {})  37.6 us
    all_to_all x2, blocking collectives, from_everyone(): return lax.all_to_all(copies, axis, split_axis=0, concat_axis=0, tiled=True)  11.9 us
    all_to_all x1, waiting for transfers between devices, summed_on_arrival(): lax.all_to_all(tiles, axis, split_axis=0, concat_axis=0, tiled=True)  5.21 us
  transfers between devices with their start and end apart: 3, of which 3 were waited for; matrix products, arithmetic and copies ran while one was open for 0% of the time, Pallas kernels for 0%

commit v1 on v0

--- a/solution.py
+++ b/solution.py
@@ -4,6 +4,12 @@
 from jax.sharding import PartitionSpec as P
 
 D = 16384
+
+
+def gather_by_exchange(x, axis, dim):
+    length = lax.axis_size(axis)
+    repeats = [length if d == dim else 1 for d in range(x.ndim)]
+    return lax.all_to_all(jnp.tile(x, repeats), axis, split_axis=dim, concat_axis=dim, tiled=True)
 
 
 def in_blocks(array, dim, devices):
@@ -81,9 +87,7 @@
     gathered_two = collect(quantized, "tr", 1)
     gathered_four = collect(gathered_two, "tq", 1)
     projected = jnp.dot(
-        lax.all_gather(gathered_four, "tp", axis=1, tiled=True),
-        q_weight,
-        preferred_element_type=jnp.float32,
+        gather_by_exchange(gathered_four, "tp", 1), q_weight, preferred_element_type=jnp.float32
     )
     query = (projected * ((peak_value + 1e-06) / 448.0)[:, None]).astype(jnp.bfloat16)
     return (hidden, peak_value, query)

time: 253 us -> 286 us (1.13)
  blocking collectives: 53.3 us -> 159 us
  waiting for transfers between devices: 167 us -> 97.9 us
    all_to_all x0 -> x1, blocking collectives: none -> 106 us  [gather_by_exchange(): lax.all_to_all(jnp.tile(x, repeats), axis, split_axis=dim, concat_axis=di...]
    all_gather x1 -> x0, waiting for transfers between devices: 69.2 us -> none  [body(): lax.all_gather(gathered_four, 'tp', axis=1, tiled=True)]
  transfers between devices with their start and end apart: 3 -> 2, of which waited for: 3 -> 2; matrix products, arithmetic and copies ran while one was open for 0% -> 0% of each run, Pallas kernels for 0% -> 0%
where the time goes in v1:
time: 286 us
  blocking collectives  159 us (56%)
  waiting for transfers between devices  97.9 us (34%)
  between operations  14.2 us (5%)
  matrix products  6.28 us (2%)
  starting transfers between devices  5.09 us (2%)
  local copies, waits for them, and re-layouts  2.9 us (1%)
    all_to_all x1, blocking collectives, gather_by_exchange(): lax.all_to_all(jnp.tile(x, repeats), axis, split_axis=dim, concat_axis=di...  106 us
    reduce_scatter x1, waiting for transfers between devices, body(): section_one = lax.psum_scatter(terms, 'tp', scatter_dimension=1, tiled=True)  92.7 us
    all_gather x3, blocking collectives, collected_together(): both, at, found = (lax.all_gather(jnp.concatenate(lines), axis), 0, {})  37.6 us
    all_to_all x2, blocking collectives, from_everyone(): return lax.all_to_all(copies, axis, split_axis=0, concat_axis=0, tiled=True)  11.9 us
  transfers between devices with their start and end apart: 2, of which 2 were waited for; matrix products, arithmetic and copies ran while one was open for 0% of the time, Pallas kernels for 0%

profile of v1, /device:TPU:34, one launch (start us, length us, event | category | flops | bytes accessed | tf_op | source)
XLA Modules:
  0.0 285.6 jit_solution(1174764520111062832)
XLA Ops:
  7.2 0.0 copy-start
  7.2 0.1 reduce-scatter.2.cloned.1.call-start
  7.3 0.6 copy-done
  7.9 4.8 %fusion.15 = f32[64,16384]{1,0:T(8,128)} fusion(bf16[64,128]{1,0:T(8,128)(2,1)S(1)} %copy-done, bf16[128,16384]{1,0:T(8,128)(2,1)} %param.7), kind=kOutput, calls=%fused_computation.64 | convolution fusion | flops 268435456 | bytes 8404992 | tf_op jit(solution)/shard_map/dot_general | solution.py:73
  12.7 0.1 reduce-scatter.2.cloned.1.call-update
  12.8 92.7 %reduce-scatter.2.cloned.1.call-done = f32[64,1024]{1,0:T(8,128)} async-done(((f32[64,16384]{1,0:T(8,128)}), f32[64,1024]{1,0:T(8,128)}) %reduce-scatter.2.cloned.1.call-update) | async-done | bytes 262160 | tf_op jit(solution)/shard_map/reduce_scatter | solution.py:74
  105.5 1.7 copy.22
  107.1 5.0 %all-to-all-start = ((f32[4,64,256]{2,1,0:T(8,128)}), f32[4,64,256]{2,1,0:T(8,128)S(1)}, u32[]{:S(2)}, u32[]{:S(2)}) async-start(f32[4,64,256]{2,1,0:T(8,128)} %bitcast.46), calls=%async_computation.1 | async-start | bytes 524288 | tf_op jit(solution)/shard_map/all_to_all | solution.py:23
  112.2 5.2 %all-to-all-done = f32[4,64,256]{2,1,0:T(8,128)S(1)} async-done(((f32[4,64,256]{2,1,0:T(8,128)}), f32[4,64,256]{2,1,0:T(8,128)S(1)}, u32[]{:S(2)}, u32[]{:S(2)}) %all-to-all-start) | async-done | bytes 262176 | tf_op jit(solution)/shard_map/all_to_all | solution.py:23
  117.4 3.8 %all_to_all.29 = f32[2,64,128]{2,1,0:T(8,128)S(1)} all-to-all(f32[2,64,128]{2,1,0:T(8,128)S(1)} %copy.12), channel_id=1, replica_groups=mesh['groups'=2,'tp'=16,'tq'=4,'tr'=2] {'tr'}, dimensions={0} | all-to-all | bytes 131072 | tf_op jit(solution)/shard_map/all_to_all | solution.py:23
  121.3 0.1 fusion.6
  121.4 0.0 copy-start.2
  121.4 27.3 %all-gather.3 = f32[16,2,64]{2,1,0:T(2,128)S(1)} all-gather(f32[1,2,64]{2,1,0:T(2,128)S(1)} %maximum_bitcast_fusion), channel_id=2, replica_groups=mesh['groups'=2,'tp'=16,'tq'=4,'tr'=2] {'tp'}, dimensions={0}, use_global_device_ids=true | all-gather | bytes 8704 | tf_op jit(solution)/shard_map/all_gather | solution.py:35
  148.7 8.5 %all-gather.4 = f32[4,2,64]{2,1,0:T(2,128)S(1)} all-gather(f32[1,2,64]{2,1,0:T(2,128)S(1)} %maximum_bitcast_fusion.1), channel_id=3, replica_groups=mesh['groups'=2,'tp'=16,'tq'=4,'tr'=2] {'tq'}, dimensions={0}, use_global_device_ids=true | all-gather | bytes 2560 | tf_op jit(solution)/shard_map/all_gather | solution.py:35
  157.3 1.9 all-gather.5
  159.1 0.0 copy-start.4
  159.1 0.1 fusion.5
  159.2 3.8 %all_to_all.30 = bf16[2,64,128]{2,1,0:T(8,128)(2,1)S(1)} all-to-all(bf16[2,64,128]{2,1,0:T(8,128)(2,1)S(1)} %broadcast_in_dim.4), channel_id=1, replica_groups=mesh['groups'=2,'tp'=16,'tq'=4,'tr'=2] {'tr'}, dimensions={0} | all-to-all | bytes 65536 | tf_op jit(solution)/shard_map/all_to_all | solution.py:61
  163.0 8.1 %all_to_all.31 = bf16[4,64,256]{2,1,0:T(8,128)(2,1)S(1)} all-to-all(bf16[4,64,256]{2,1,0:T(8,128)(2,1)S(1)} %broadcast_in_dim.5), channel_id=1, replica_groups=mesh['groups'=2,'tp'=16,'tq'=4,'tr'=2] {'tq'}, dimensions={0} | all-to-all | bytes 262144 | tf_op jit(solution)/shard_map/all_to_all | solution.py:61
  171.1 0.3 tile.9
  171.4 0.0 copy-start.1
  171.4 105.6 %all_to_all.32 = bf16[64,16,1024]{2,0,1:T(8,128)(2,1)S(1)} all-to-all(bf16[64,16,1024]{2,0,1:T(8,128)(2,1)S(1)} %tile.9), channel_id=1, replica_groups=mesh['groups'=2,'tp'=16,'tq'=4,'tr'=2] {'tp'}, dimensions={1} | all-to-all | bytes 4194304 | tf_op jit(solution)/shard_map/all_to_all | solution.py:12
  277.0 0.2 copy.19
  277.3 1.5 fusion
  (24 shorter events, 0.2 us)
Async XLA Ops:
  7.2 0.7 copy-start
  7.2 98.3 %reduce-scatter.2.cloned.1.call-start = ((), (), s32[]{:S(2)}) async-start(), calls=%async_computation.6 | async-start | bytes 4456448 | tf_op jit(solution)/shard_map/reduce_scatter | solution.py:74
  12.7 99.4 %copy-start.5 = (bf16[128]{0:T(256)(128)(2,1)S(1)}, bf16[128]{0:T(256)(128)(2,1)}, u32[]{:S(2)}) copy-start(bf16[128]{0:T(256)(128)(2,1)} %param.8) | copy-start | bytes 772
  12.7 108.5 %copy-start.3 = (bf16[64,128]{1,0:T(8,128)(2,1)S(1)}, bf16[64,128]{1,0:T(8,128)(2,1)}, u32[]{:S(2)}) copy-start(bf16[64,128]{1,0:T(8,128)(2,1)} %param.6) | copy-start | bytes 49156
  107.1 10.3 %all-to-all-start = ((f32[4,64,256]{2,1,0:T(8,128)}), f32[4,64,256]{2,1,0:T(8,128)S(1)}, u32[]{:S(2)}, u32[]{:S(2)}) async-start(f32[4,64,256]{2,1,0:T(8,128)} %bitcast.46), calls=%async_computation.1 | async-start | bytes 524288 | tf_op jit(solution)/shard_map/all_to_all | solution.py:23
  121.4 155.9 %copy-start.2 = (bf16[64,128]{1,0:T(8,128)(2,1)}, bf16[64,128]{1,0:T(8,128)(2,1)S(1)}, u32[]{:S(2)}) copy-start(bf16[64,128]{1,0:T(8,128)(2,1)S(1)} %get-tuple-element.8) | copy-start | bytes 49156
  159.1 118.1 %copy-start.4 = (f32[64]{0:T(128)}, f32[64]{0:T(128)S(1)}, u32[]{:S(2)}) copy-start(f32[64]{0:T(128)S(1)} %get-tuple-element.6) | copy-start | bytes 772
  171.4 105.9 %copy-start.1 = (bf16[16384,128]{1,0:T(8,128)(2,1)S(1)}, bf16[16384,128]{1,0:T(8,128)(2,1)}, u32[]{:S(2)}) copy-start(bf16[16384,128]{1,0:T(8,128)(2,1)} %param.9) | copy-start | bytes 12582916
Sparse Core Ops, SparseCore 0:
  12.9 92.5 reduce-scatter.1
